TPU v7x, 256 devices: a whole 4x4x8 slice. The times are simulated.
256 devices in a mesh: seq: 64 (over z, x, core), head: 4 (over y).
Axes of the slice: x: 4, y: 4, z: 8, core: 2. Of those that a mesh axis runs over, the one named last changes fastest.
Arguments:
- query: bfloat16 [32768, 4096], P(('seq', 'head')), may hold values from -6 to 6
- key: bfloat16 [32768, 1024], P(('seq', 'head')), may hold values from -6 to 6
- value: bfloat16 [32768, 1024], P(('seq', 'head')), may hold values from -6 to 6
- out: bfloat16 [32768, 4096], P(('seq', 'head')), may hold values from -4 to 4
- output_gradient: bfloat16 [32768, 4096], P(('seq', 'head')), may hold values from -6 to 6
- log_sum_exp: float32 [32768, 32], P(('seq', 'head')), may hold values from 4 to 7
- segment_ids: int32 [32768], replicated, may hold values from 0 to 31, never falling along the last dimension, each value on 1 to 1536 neighbouring positions
Outputs:
- d_query: bfloat16 [32768, 4096], P(('seq', 'head'))
- key_gradient: bfloat16 [32768, 1024], P(('seq', 'head'))
- value_gradient: bfloat16 [32768, 1024], P(('seq', 'head'))
Inputs may be any that keep to these rules, and one draw needn't show every extreme that they name: `segment_ids`: never falls along the positions; a document holds at most 1536 positions, and one holds exactly 1536.
All inputs are finite; a program needn't handle non-finite values.
Results may differ from a plain program's by a relative error of at most 0.0071.
Values may be sent and summed in bfloat16 or wider, within the bound.
A program may use at most 128 MiB of HBM per device.

v0:
```python
import functools
import math

import jax
import jax.numpy as jnp
from jax import lax
from jax.experimental import pallas as pl
from jax.experimental.pallas import tpu as pltpu
from jax.sharding import PartitionSpec as P

MESH = pl.DeviceIdType.MESH
BF16 = jnp.bfloat16
F32 = jnp.float32

HEAD = 128
TOK = 128
GROUP = 4
Y = 4
PIECES = 8
SPAN = PIECES * TOK
HALF = SPAN // 2
HALO = SPAN + HALF
BLOCK = 256
HALO_BLOCKS = HALO // BLOCK
SPAN_BLOCKS = SPAN // BLOCK
QCOLS = GROUP * HEAD

LOG2E = math.log2(math.e)
SCALE = 1.0 / math.sqrt(HEAD)
SHIFT = 4.0
REST = SCALE * 2.0**SHIFT
NT = (((1,), (1,)), ((), ()))
TN = (((0,), (0,)), ((), ()))


def kernel(
    n_span,
    q_hbm, k_hbm, v_hbm, o_hbm, e_hbm, lse_ref, seg_ref,
    dq_out, dk_out, dv_out,
    k_src, v_src, o_src, e_src, aux_src,
    k_all, v_all, q_all, e_all, aux, seg_k, seg_q,
    dq_t, dk_acc, dv_acc,
    dq_send, dk_send, dv_send, dk_back, dv_back, dk_near, dv_near, dk_far, dv_far,
    load_sem, kv_send, kv_recv, aux_send, aux_recv, qe_send, qe_recv,
    halo_send, halo_recv, back_send, back_recv, out_send, out_recv,
):
    seq = lax.axis_index("seq")
    y = lax.axis_index("head")
    span = lax.div(seq, 2)
    core = lax.rem(seq, 2)
    mine = core * Y + y
    group = y * 2 + core

    def piece_device(piece):
        return (span * 2 + piece // Y, piece % Y)

    def span_device(by):
        return (seq + 2 * by, y)

    peers = []
    for dy in (1, 3, 2, 0):
        for dcore in (0, 1):
            if dy or dcore:
                py = lax.rem(y + dy, Y)
                pcore = lax.rem(core + dcore, 2)
                peers.append((dy * 2 + dcore, (span * 2 + pcore, py), py * 2 + pcore))

    has_prev, has_prev2 = span >= 1, span >= 2
    has_next, has_next2 = span < n_span - 1, span < n_span - 2

    def cols(g, width):
        return pl.ds(pl.multiple_of(g * width, width), width)

    my_rows = pl.ds(pl.multiple_of(mine * TOK, TOK), TOK)
    my_key_rows = pl.ds(pl.multiple_of(HALO + mine * TOK, TOK), TOK)
    loads = [
        pltpu.make_async_copy(src, dst, load_sem.at[i])
        for i, (src, dst) in enumerate(
            ((k_hbm, k_src), (v_hbm, v_src), (e_hbm, e_src), (o_hbm, o_src))
        )
    ]
    own = [
        pltpu.make_async_copy(k_hbm.at[:, cols(group, HEAD)], k_all.at[my_key_rows, :], kv_recv.at[0, mine]),
        pltpu.make_async_copy(v_hbm.at[:, cols(group, HEAD)], v_all.at[my_key_rows, :], kv_recv.at[1, mine]),
    ]
    for h in range(GROUP):
        columns = pl.ds(pl.multiple_of(group * QCOLS + h * HEAD, HEAD), HEAD)
        for i, (src, dst) in enumerate(((q_hbm, q_all), (e_hbm, e_all))):
            own.append(
                pltpu.make_async_copy(
                    src.at[:, columns], dst.at[my_rows, pl.ds(h * HEAD, HEAD)], qe_recv.at[i, h, mine]
                )
            )
    for copy in loads + own:
        copy.start()

    barrier = pltpu.get_barrier_semaphore()

    def greet(device):
        pl.semaphore_signal(barrier, inc=1, device_id=device, device_id_type=MESH)

    for _, device, _ in peers:
        greet(device)
    pl.when(has_prev)(lambda: greet(span_device(-1)))
    pl.when(has_prev2)(lambda: greet(span_device(-2)))
    pl.when(has_next)(lambda: greet(span_device(1)))
    pl.when(has_next2)(lambda: greet(span_device(2)))
    neighbours = jnp.minimum(span, 2) + jnp.minimum(n_span - 1 - span, 2)
    pl.semaphore_wait(barrier, len(peers) + neighbours)

    def remote(src, dst, send, recv, device):
        return pltpu.make_async_remote_copy(
            src_ref=src, dst_ref=dst, send_sem=send, recv_sem=recv, device_id=device, device_id_type=MESH
        )

    sends = []
    loads[0].wait()
    loads[1].wait()
    for n, device, g in peers:
        for i, (src, dst) in enumerate(((k_src, k_all), (v_src, v_all))):
            sends.append(
                remote(src.at[:, cols(g, HEAD)], dst.at[my_key_rows, :], kv_send.at[i, n], kv_recv.at[i, mine], device)
            )
            sends[-1].start()

    loads[2].wait()
    for h in range(GROUP):
        for n, device, g in peers:
            columns = pl.ds(pl.multiple_of(g * QCOLS + h * HEAD, HEAD), HEAD)
            for i, (src, dst) in enumerate(((q_hbm, q_all), (e_src, e_all))):
                sends.append(
                    remote(
                        src.at[:, columns], dst.at[my_rows, pl.ds(h * HEAD, HEAD)],
                        qe_send.at[i, h, n], qe_recv.at[i, h, mine], device,
                    )
                )
                sends[-1].start()
        if h == 0:
            loads[3].wait()
            lane = lax.broadcasted_iota(jnp.int32, (TOK, HEAD), 1)
            delta = jnp.zeros((TOK, HEAD), F32)
            for head in range(PIECES * GROUP):
                part = pl.ds(head * HEAD, HEAD)
                product = e_src[:, part].astype(F32) * o_src[:, part].astype(F32)
                delta = jnp.where(lane == head, jnp.sum(product, axis=1, keepdims=True), delta)
            delta = delta.T
            lse = jnp.concatenate([lse_ref[...], jnp.zeros((TOK, HEAD - PIECES * GROUP), F32)], axis=1).T
            lse = lse * LOG2E + SHIFT
            for g in range(PIECES):
                aux_src[g, 0:GROUP, :] = lse[g * GROUP : (g + 1) * GROUP, :]
                aux_src[g, GROUP : 2 * GROUP, :] = delta[g * GROUP : (g + 1) * GROUP, :]
            for n, device, g in peers:
                sends.append(remote(aux_src.at[g], aux.at[mine], aux_send.at[n], aux_recv.at[mine], device))
                sends[-1].start()
            aux[mine] = aux_src[group]

    first = span * PIECES - HALO // TOK
    for i in range((HALO + SPAN) // TOK):
        row = seg_ref[pl.ds(jnp.maximum(first + i, 0), 1), :]
        row = jnp.where(first + i < 0, -1, row)
        seg_k[pl.ds(i * TOK, TOK), :] = jnp.broadcast_to(row, (TOK, TOK)).T
        if i >= HALO // TOK:
            seg_q[:, pl.ds(i * TOK - HALO, TOK)] = row

    dk_acc[...] = jnp.zeros_like(dk_acc)
    dv_acc[...] = jnp.zeros_like(dv_acc)
    dq_t[...] = jnp.zeros_like(dq_t)

    def halo_copies(by, piece):
        rows = pl.ds(HALO + piece * TOK, TOK)
        to = pl.ds((HALF if by == 1 else -HALF) + piece * TOK, TOK)
        at = piece if by == 1 else piece + Y
        return [
            remote(ref.at[rows, :], ref.at[to, :], halo_send.at[i, at], halo_recv.at[i, at], span_device(by))
            for i, ref in enumerate((k_all, v_all))
        ]

    def start_all(copies):
        for copy in copies:
            copy.start()

    def here(ref, sem):
        return pltpu.make_async_copy(ref, ref, sem)

    for piece in reversed(range(PIECES)):
        rows = pl.ds(HALO + piece * TOK, TOK)
        here(k_all.at[rows, :], kv_recv.at[0, piece]).wait()
        here(v_all.at[rows, :], kv_recv.at[1, piece]).wait()
        pl.when(has_next)(lambda: start_all(halo_copies(1, piece)))
        if piece >= Y:
            pl.when(has_next2)(lambda: start_all(halo_copies(2, piece)))

    for piece in range(PIECES):
        pl.when(mine != piece)(lambda: here(aux.at[piece], aux_recv.at[piece]).wait())

    def step(j, h, r0, r1):
        keys = pl.ds(j * BLOCK, BLOCK)
        width = (r1 - r0) * BLOCK
        rows = pl.ds(r0 * BLOCK, width)
        columns = pl.ds(pl.multiple_of(h * HEAD, HEAD), HEAD)
        q, e = q_all[rows, columns], e_all[rows, columns]
        k, v = k_all[keys, :], v_all[keys, :]
        scores = lax.dot_general(k, q, NT, preferred_element_type=F32)
        dprobs = lax.dot_general(v, e, NT, preferred_element_type=F32)
        pieces = range(r0 * BLOCK // TOK, r1 * BLOCK // TOK)
        lse = jnp.concatenate([aux[p, pl.ds(h, 1), :] for p in pieces], axis=1)
        delta = jnp.concatenate([aux[p, pl.ds(h + GROUP, 1), :] for p in pieces], axis=1)
        doc = jnp.concatenate([seg_k[keys, :]] * (width // TOK), axis=1)
        allowed = doc == seg_q[:, rows]
        if j >= HALO_BLOCKS:
            key_at = lax.broadcasted_iota(jnp.int32, (BLOCK, width), 0) + (j - HALO_BLOCKS) * BLOCK
            query_at = lax.broadcasted_iota(jnp.int32, (BLOCK, width), 1) + r0 * BLOCK
            allowed = allowed & (key_at <= query_at)
        probs = jnp.exp2(jnp.where(allowed, scores * (SCALE * LOG2E) - lse, -jnp.inf))
        dscores = (probs * (dprobs - delta)).astype(BF16)
        probs = probs.astype(BF16)
        dv_acc[keys, :] += jnp.dot(probs, e, preferred_element_type=F32)
        dk_acc[keys, :] += jnp.dot(dscores, q, preferred_element_type=F32)
        dq_t[h, :, rows] += lax.dot_general(k, dscores, TN, preferred_element_type=F32)

    def own_head(h, carry):
        for piece in range(PIECES):
            rows = pl.ds(piece * TOK, TOK)
            columns = pl.ds(pl.multiple_of(h * HEAD, HEAD), HEAD)
            here(q_all.at[rows, columns], qe_recv.at[0, h, piece]).wait()
            here(e_all.at[rows, columns], qe_recv.at[1, h, piece]).wait()
        for b in range(SPAN_BLOCKS):
            step(HALO_BLOCKS + b, h, b, SPAN_BLOCKS)
        return carry

    lax.fori_loop(0, GROUP, own_head, 0)

    def dq_copy(piece):
        return remote(
            dq_send.at[pl.ds(piece * TOK, TOK), :], dq_out.at[:, cols(group, QCOLS)],
            out_send.at[0, piece], out_recv.at[0, group], piece_device(piece),
        )

    def dq_local(piece):
        return pltpu.make_async_copy(
            dq_send.at[pl.ds(piece * TOK, TOK), :], dq_out.at[:, cols(group, QCOLS)], out_recv.at[0, group]
        )

    def finish_rows(r):
        rows = pl.ds(r * BLOCK, BLOCK)
        for h in range(GROUP):
            dq_send[rows, pl.ds(h * HEAD, HEAD)] = (dq_t[h, :, rows].T * REST).astype(BF16)
        for piece in (2 * r, 2 * r + 1):
            pl.when(mine != piece)(lambda: dq_copy(piece).start())
            pl.when(mine == piece)(lambda: dq_local(piece).start())

    def back_copies(j):
        rows = pl.ds(j * BLOCK, BLOCK)
        if j * BLOCK >= HALF:
            dsts, at, by = (dk_near, dv_near), pl.ds(j * BLOCK - HALF, BLOCK), -1
        else:
            dsts, at, by = (dk_far, dv_far), rows, -2
        return [
            remote(src.at[rows, :], dst.at[at, :], back_send.at[i, j], back_recv.at[i, j], span_device(by))
            for i, (src, dst) in enumerate(((dk_back, dsts[0]), (dv_back, dsts[1])))
        ]

    def halo_block(j):
        rows = pl.ds(j * BLOCK, BLOCK)
        far = j * BLOCK < HALF
        for piece in (2 * j, 2 * j + 1):
            at = (piece + PIECES) if far else piece - Y
            at_rows = pl.ds(piece * TOK, TOK)
            here(k_all.at[at_rows, :], halo_recv.at[0, at]).wait()
            here(v_all.at[at_rows, :], halo_recv.at[1, at]).wait()

        def head(h, carry):
            step(j, h, max(0, j - HALO_BLOCKS), min(SPAN_BLOCKS, j + 1))
            return carry

        lax.fori_loop(0, GROUP, head, 0)
        dk_back[rows, :] = (dk_acc[rows, :] * REST).astype(BF16)
        dv_back[rows, :] = (dv_acc[rows, :] * 2.0**SHIFT).astype(BF16)
        start_all(back_copies(j))

    for j in reversed(range(HALO_BLOCKS)):
        pl.when(has_prev if j * BLOCK >= HALF else has_prev2)(lambda: halo_block(j))
        if j < SPAN_BLOCKS:
            finish_rows(j)

    def dkv_copies(piece):
        rows = pl.ds(piece * TOK, TOK)
        return [
            remote(
                src.at[rows, :], dst.at[:, cols(group, HEAD)],
                out_send.at[i, piece], out_recv.at[i, group], piece_device(piece),
            )
            for i, src, dst in ((1, dk_send, dk_out), (2, dv_send, dv_out))
        ]

    def dkv_local(piece):
        rows = pl.ds(piece * TOK, TOK)
        return [
            pltpu.make_async_copy(src.at[rows, :], dst.at[:, cols(group, HEAD)], out_recv.at[i, group])
            for i, src, dst in ((1, dk_send, dk_out), (2, dv_send, dv_out))
        ]

    def finish_keys(b):
        rows = pl.ds(b * BLOCK, BLOCK)
        acc_rows = pl.ds(HALO + b * BLOCK, BLOCK)
        for i, acc, near, far, out, factor in (
            (0, dk_acc, dk_near, dk_far, dk_send, REST),
            (1, dv_acc, dv_near, dv_far, dv_send, 2.0**SHIFT),
        ):
            acc[acc_rows, :] *= factor

            def add_near():
                here(near.at[rows, :], back_recv.at[i, b + HALF // BLOCK]).wait()
                acc[acc_rows, :] += near[rows, :].astype(F32)

            def add_far():
                far_rows = pl.ds(b * BLOCK - HALF, BLOCK)
                here(far.at[far_rows, :], back_recv.at[i, b - HALF // BLOCK]).wait()
                acc[acc_rows, :] += far[far_rows, :].astype(F32)

            pl.when(has_next)(add_near)
            if b * BLOCK >= HALF:
                pl.when(has_next2)(add_far)
            out[rows, :] = acc[acc_rows, :].astype(BF16)
        for piece in (2 * b, 2 * b + 1):
            pl.when(mine != piece)(lambda: start_all(dkv_copies(piece)))
            pl.when(mine == piece)(lambda: start_all(dkv_local(piece)))

    for b in (1, 0, 3, 2):
        finish_keys(b)

    for g in range(PIECES):
        here(dq_out.at[:, pl.ds(g * QCOLS, QCOLS)], out_recv.at[0, g]).wait()
        here(dk_out.at[:, pl.ds(g * HEAD, HEAD)], out_recv.at[1, g]).wait()
        here(dv_out.at[:, pl.ds(g * HEAD, HEAD)], out_recv.at[2, g]).wait()
    for copy in sends:
        copy.wait_send()

    def wait_sends(copies):
        for copy in copies:
            copy.wait_send()

    for piece in range(PIECES):
        pl.when(has_next)(lambda: wait_sends(halo_copies(1, piece)))
        if piece >= Y:
            pl.when(has_next2)(lambda: wait_sends(halo_copies(2, piece)))
        pl.when(mine != piece)(lambda: wait_sends([dq_copy(piece)] + dkv_copies(piece)))
    for j in range(HALO_BLOCKS):
        pl.when(has_prev if j * BLOCK >= HALF else has_prev2)(lambda: wait_sends(back_copies(j)))


def shards(n_span, query, key, value, out, output_gradient, log_sum_exp, segment_ids):
    any_space = pl.BlockSpec(memory_space=pl.ANY)
    vmem = pl.BlockSpec(memory_space=pltpu.VMEM)
    dma = pltpu.SemaphoreType.DMA
    shape = jax.ShapeDtypeStruct
    window = HALO + SPAN
    return pl.pallas_call(
        functools.partial(kernel, n_span),
        out_shape=[
            shape(query.shape, BF16),
            shape(key.shape, BF16),
            shape(value.shape, BF16),
        ],
        in_specs=[any_space] * 5 + [vmem] * 2,
        out_specs=[any_space] * 3,
        scratch_shapes=[
            pltpu.VMEM((TOK, PIECES * HEAD), BF16),
            pltpu.VMEM((TOK, PIECES * HEAD), BF16),
            pltpu.VMEM((TOK, PIECES * QCOLS), BF16),
            pltpu.VMEM((TOK, PIECES * QCOLS), BF16),
            pltpu.VMEM((PIECES, 2 * GROUP, TOK), F32),
            pltpu.VMEM((window, HEAD), BF16),
            pltpu.VMEM((window, HEAD), BF16),
            pltpu.VMEM((SPAN, QCOLS), BF16),
            pltpu.VMEM((SPAN, QCOLS), BF16),
            pltpu.VMEM((PIECES, 2 * GROUP, TOK), F32),
            pltpu.VMEM((window, TOK), jnp.int32),
            pltpu.VMEM((1, SPAN), jnp.int32),
            pltpu.VMEM((GROUP, HEAD, SPAN), F32),
            pltpu.VMEM((window, HEAD), F32),
            pltpu.VMEM((window, HEAD), F32),
            pltpu.VMEM((SPAN, QCOLS), BF16),
            pltpu.VMEM((SPAN, HEAD), BF16),
            pltpu.VMEM((SPAN, HEAD), BF16),
            pltpu.VMEM((HALO, HEAD), BF16),
            pltpu.VMEM((HALO, HEAD), BF16),
            pltpu.VMEM((SPAN, HEAD), BF16),
            pltpu.VMEM((SPAN, HEAD), BF16),
            pltpu.VMEM((HALF, HEAD), BF16),
            pltpu.VMEM((HALF, HEAD), BF16),
            dma((4,)),
            dma((2, PIECES)),
            dma((2, PIECES)),
            dma((PIECES,)),
            dma((PIECES,)),
            dma((2, GROUP, PIECES)),
            dma((2, GROUP, PIECES)),
            dma((2, PIECES + Y)),
            dma((2, PIECES + Y)),
            dma((2, HALO_BLOCKS)),
            dma((2, HALO_BLOCKS)),
            dma((3, PIECES)),
            dma((3, PIECES)),
        ],
        name="attention_backward",
        compiler_params=pltpu.CompilerParams(
            collective_id=0, has_side_effects=True, vmem_limit_bytes=48 * 2**20
        ),
    )(query, key, value, out, output_gradient, log_sum_exp, segment_ids.reshape(-1, TOK))


def solution(mesh):
    rows = P(("seq", "head"), None)
    return jax.shard_map(
        functools.partial(shards, mesh.shape["seq"] // 2),
        mesh=mesh,
        in_specs=(rows,) * 6 + (P(),),
        out_specs=(rows,) * 3,
        check_vma=False,
    )
```

profile of v0, /device:TPU:103, one launch (start us, length us, event | category | flops | bytes accessed | tf_op | source)
XLA Modules:
  0.0 83.7 jit_solution(5859238076869746460)
XLA Ops:
  0.6 0.8 copy.10.lse_ref
  1.4 0.0 copy-start
  1.5 1.2 %copy-done = bf16[128,4096]{1,0:T(8,128)(2,1)S(1)} copy-done((bf16[128,4096]{1,0:T(8,128)(2,1)S(1)}, bf16[128,4096]{1,0:T(8,128)(2,1)}, u32[]{:S(2)}) %copy-start) | copy-done | bytes 1048600
  2.7 0.0 copy-start.1
  2.7 1.2 %copy-done.1 = bf16[128,4096]{1,0:T(8,128)(2,1)S(1)} copy-done((bf16[128,4096]{1,0:T(8,128)(2,1)S(1)}, bf16[128,4096]{1,0:T(8,128)(2,1)}, u32[]{:S(2)}) %copy-start.1) | copy-done | bytes 1048600
  3.9 0.0 copy-start.2
  3.9 1.2 %copy-done.2 = bf16[128,4096]{1,0:T(8,128)(2,1)S(1)} copy-done((bf16[128,4096]{1,0:T(8,128)(2,1)S(1)}, bf16[128,4096]{1,0:T(8,128)(2,1)}, u32[]{:S(2)}) %copy-start.2) | copy-done | bytes 1048600
  5.1 0.0 copy-start.3
  5.1 0.9 %copy-done.3 = bf16[128,1024]{1,0:T(8,128)(2,1)S(1)} copy-done((bf16[128,1024]{1,0:T(8,128)(2,1)S(1)}, bf16[128,1024]{1,0:T(8,128)(2,1)}, u32[]{:S(2)}) %copy-start.3) | copy-done | bytes 262168
  6.1 0.0 copy-start.4
  6.1 0.9 %copy-done.4 = bf16[128,1024]{1,0:T(8,128)(2,1)S(1)} copy-done((bf16[128,1024]{1,0:T(8,128)(2,1)S(1)}, bf16[128,1024]{1,0:T(8,128)(2,1)}, u32[]{:S(2)}) %copy-start.4) | copy-done | bytes 262168
  7.0 0.0 copy-start.5
  7.0 0.9 %copy-done.5 = s32[32768]{0:T(1024)S(1)} copy-done((s32[32768]{0:T(1024)S(1)}, s32[32768]{0:T(1024)}, u32[]{:S(2)}) %copy-start.5) | copy-done | bytes 131096
  7.9 73.4 %attention_backward.1 = (bf16[128,4096]{1,0:T(8,128)(2,1)S(1)}, bf16[128,1024]{1,0:T(8,128)(2,1)S(1)}, bf16[128,1024]{1,0:T(8,128)(2,1)S(1)}) custom-call(bf16[128,4096]{1,0:T(8,128)(2,1)S(1)} %copy-done, bf16[128,1024]{1,0:T(8,128)(2,1)S(1)} %copy-done.3, bf16[128,1024]{1,0:T(8,128)(2,1)S(1)} %copy-done.4, bf16[128,4096]{1,0:T(8,128)(2,1)S(1)} %copy-done.1, ...), custom_call_target="tpu_custom_call" | custom-call | tf_op jit(solution)/shard_map/attention_backward/pallas_call | solution.py:358
  81.3 1.0 %copy.14 = bf16[128,4096]{1,0:T(8,128)(2,1)} copy(bf16[128,4096]{1,0:T(8,128)(2,1)S(1)} %get-tuple-element.6) | data formatting | bytes 2097152
  82.3 0.7 copy.15
  83.0 0.7 copy.16
Async XLA Ops:
  1.4 1.2 %copy-start = (bf16[128,4096]{1,0:T(8,128)(2,1)S(1)}, bf16[128,4096]{1,0:T(8,128)(2,1)}, u32[]{:S(2)}) copy-start(bf16[128,4096]{1,0:T(8,128)(2,1)} %q_hbm.1) | copy-start | bytes 3145732
  2.7 1.2 %copy-start.1 = (bf16[128,4096]{1,0:T(8,128)(2,1)S(1)}, bf16[128,4096]{1,0:T(8,128)(2,1)}, u32[]{:S(2)}) copy-start(bf16[128,4096]{1,0:T(8,128)(2,1)} %o_hbm.1) | copy-start | bytes 3145732
  3.9 1.2 %copy-start.2 = (bf16[128,4096]{1,0:T(8,128)(2,1)S(1)}, bf16[128,4096]{1,0:T(8,128)(2,1)}, u32[]{:S(2)}) copy-start(bf16[128,4096]{1,0:T(8,128)(2,1)} %e_hbm.1) | copy-start | bytes 3145732
  5.1 0.9 %copy-start.3 = (bf16[128,1024]{1,0:T(8,128)(2,1)S(1)}, bf16[128,1024]{1,0:T(8,128)(2,1)}, u32[]{:S(2)}) copy-start(bf16[128,1024]{1,0:T(8,128)(2,1)} %k_hbm.1) | copy-start | bytes 786436
  6.1 0.9 %copy-start.4 = (bf16[128,1024]{1,0:T(8,128)(2,1)S(1)}, bf16[128,1024]{1,0:T(8,128)(2,1)}, u32[]{:S(2)}) copy-start(bf16[128,1024]{1,0:T(8,128)(2,1)} %v_hbm.1) | copy-start | bytes 786436
  7.0 0.9 %copy-start.5 = (s32[32768]{0:T(1024)S(1)}, s32[32768]{0:T(1024)}, u32[]{:S(2)}) copy-start(s32[32768]{0:T(1024)} %param.13) | copy-start | bytes 393220
where the time goes:
time: 84.1 us; the launch traced here: 83.7 us
  Pallas kernels  73.4 us (87%)
  local copies, waits for them, and re-layouts  9.66 us (11%)
    pallas_call x1, Pallas kernels, shards(): pl.pallas_call(functools.partial(kernel, n_span), out_shape=[shape(query....  73.4 us
    unnamed x16, local copies, waits for them, and re-layouts  9.66 us

commit v1 on v0

--- a/solution.py
+++ b/solution.py
@@ -35,14 +35,15 @@
 
 def kernel(
     n_span,
-    q_hbm, k_hbm, v_hbm, o_hbm, e_hbm, lse_ref, seg_ref,
+    q_hbm, k_hbm, v_hbm, o_hbm, e_hbm, lse_hbm, seg_hbm,
     dq_out, dk_out, dv_out,
-    k_src, v_src, o_src, e_src, aux_src,
+    k_src, v_src, o_src, e_src, lse_ref, seg_ref, aux_src,
     k_all, v_all, q_all, e_all, aux, seg_k, seg_q,
     dq_t, dk_acc, dv_acc,
     dq_send, dk_send, dv_send, dk_back, dv_back, dk_near, dv_near, dk_far, dv_far,
     load_sem, kv_send, kv_recv, aux_send, aux_recv, qe_send, qe_recv,
-    halo_send, halo_recv, back_send, back_recv, out_send, out_recv,
+    halo_send, halo_recv, back_send, back_recv,
+    dq_send_sem, dq_recv_sem, dkv_send_sem, dkv_recv_sem,
 ):
     seq = lax.axis_index("seq")
     y = lax.axis_index("head")
@@ -76,7 +77,10 @@
     loads = [
         pltpu.make_async_copy(src, dst, load_sem.at[i])
         for i, (src, dst) in enumerate(
-            ((k_hbm, k_src), (v_hbm, v_src), (e_hbm, e_src), (o_hbm, o_src))
+            (
+                (k_hbm, k_src), (v_hbm, v_src), (e_hbm, e_src), (o_hbm, o_src),
+                (lse_hbm, lse_ref), (seg_hbm, seg_ref),
+            )
         )
     ]
     own = [
@@ -137,6 +141,7 @@
                 sends[-1].start()
         if h == 0:
             loads[3].wait()
+            loads[4].wait()
             lane = lax.broadcasted_iota(jnp.int32, (TOK, HEAD), 1)
             delta = jnp.zeros((TOK, HEAD), F32)
             for head in range(PIECES * GROUP):
@@ -144,8 +149,7 @@
                 product = e_src[:, part].astype(F32) * o_src[:, part].astype(F32)
                 delta = jnp.where(lane == head, jnp.sum(product, axis=1, keepdims=True), delta)
             delta = delta.T
-            lse = jnp.concatenate([lse_ref[...], jnp.zeros((TOK, HEAD - PIECES * GROUP), F32)], axis=1).T
-            lse = lse * LOG2E + SHIFT
+            lse = lse_ref[...] * LOG2E + SHIFT
             for g in range(PIECES):
                 aux_src[g, 0:GROUP, :] = lse[g * GROUP : (g + 1) * GROUP, :]
                 aux_src[g, GROUP : 2 * GROUP, :] = delta[g * GROUP : (g + 1) * GROUP, :]
@@ -154,6 +158,32 @@
                 sends[-1].start()
             aux[mine] = aux_src[group]
 
+    def halo_copies(by, piece):
+        rows = pl.ds(pl.multiple_of(HALO + piece * TOK, TOK), TOK)
+        to = pl.ds(pl.multiple_of((HALF if by == 1 else -HALF) + piece * TOK, TOK), TOK)
+        at = piece if by == 1 else piece + Y
+        return [
+            remote(ref.at[rows, :], ref.at[to, :], halo_send.at[i, at], halo_recv.at[i, at], span_device(by))
+            for i, ref in enumerate((k_all, v_all))
+        ]
+
+    def start_all(copies):
+        for copy in copies:
+            copy.start()
+
+    def here(ref, sem):
+        return pltpu.make_async_copy(ref, ref, sem)
+
+    for dy, dcore in ((0, 0), (0, 1), (1, 0), (3, 0), (1, 1), (3, 1), (2, 0), (2, 1)):
+        piece = lax.rem(core + dcore, 2) * Y + lax.rem(y + dy, Y)
+        rows = pl.ds(pl.multiple_of(HALO + piece * TOK, TOK), TOK)
+        here(k_all.at[rows, :], kv_recv.at[0, piece]).wait()
+        here(v_all.at[rows, :], kv_recv.at[1, piece]).wait()
+        pl.when(has_next)(lambda: start_all(halo_copies(1, piece)))
+    for piece in range(Y, PIECES):
+        pl.when(has_next2)(lambda: start_all(halo_copies(2, piece)))
+
+    loads[5].wait()
     first = span * PIECES - HALO // TOK
     for i in range((HALO + SPAN) // TOK):
         row = seg_ref[pl.ds(jnp.maximum(first + i, 0), 1), :]
@@ -165,30 +195,6 @@
     dk_acc[...] = jnp.zeros_like(dk_acc)
     dv_acc[...] = jnp.zeros_like(dv_acc)
     dq_t[...] = jnp.zeros_like(dq_t)
-
-    def halo_copies(by, piece):
-        rows = pl.ds(HALO + piece * TOK, TOK)
-        to = pl.ds((HALF if by == 1 else -HALF) + piece * TOK, TOK)
-        at = piece if by == 1 else piece + Y
-        return [
-            remote(ref.at[rows, :], ref.at[to, :], halo_send.at[i, at], halo_recv.at[i, at], span_device(by))
-            for i, ref in enumerate((k_all, v_all))
-        ]
-
-    def start_all(copies):
-        for copy in copies:
-            copy.start()
-
-    def here(ref, sem):
-        return pltpu.make_async_copy(ref, ref, sem)
-
-    for piece in reversed(range(PIECES)):
-        rows = pl.ds(HALO + piece * TOK, TOK)
-        here(k_all.at[rows, :], kv_recv.at[0, piece]).wait()
-        here(v_all.at[rows, :], kv_recv.at[1, piece]).wait()
-        pl.when(has_next)(lambda: start_all(halo_copies(1, piece)))
-        if piece >= Y:
-            pl.when(has_next2)(lambda: start_all(halo_copies(2, piece)))
 
     for piece in range(PIECES):
         pl.when(mine != piece)(lambda: here(aux.at[piece], aux_recv.at[piece]).wait())
@@ -218,36 +224,67 @@
         dk_acc[keys, :] += jnp.dot(dscores, q, preferred_element_type=F32)
         dq_t[h, :, rows] += lax.dot_general(k, dscores, TN, preferred_element_type=F32)
 
-    def own_head(h, carry):
+    def wait_head(h):
+        columns = pl.ds(pl.multiple_of(h * HEAD, HEAD), HEAD)
         for piece in range(PIECES):
             rows = pl.ds(piece * TOK, TOK)
-            columns = pl.ds(pl.multiple_of(h * HEAD, HEAD), HEAD)
             here(q_all.at[rows, columns], qe_recv.at[0, h, piece]).wait()
             here(e_all.at[rows, columns], qe_recv.at[1, h, piece]).wait()
+
+    def wait_halo(pieces, by):
+        for piece in pieces:
+            at = piece if by == 1 else piece + Y
+            rows = pl.ds((HALF if by == 1 else -HALF) + piece * TOK, TOK)
+            here(k_all.at[rows, :], halo_recv.at[0, at]).wait()
+            here(v_all.at[rows, :], halo_recv.at[1, at]).wait()
+
+    def own(h):
         for b in range(SPAN_BLOCKS):
             step(HALO_BLOCKS + b, h, b, SPAN_BLOCKS)
+
+    def halo(h, blocks):
+        for j in blocks:
+            step(j, h, 0, min(SPAN_BLOCKS, j + 1))
+
+    near_blocks = tuple(reversed(range(HALF // BLOCK, HALO_BLOCKS)))
+    far_blocks = tuple(reversed(range(HALF // BLOCK)))
+
+    def dq_copy(h, piece):
+        columns = pl.ds(pl.multiple_of(h * HEAD, HEAD), HEAD)
+        out_columns = pl.ds(pl.multiple_of(group * QCOLS + h * HEAD, HEAD), HEAD)
+        return remote(
+            dq_send.at[pl.ds(piece * TOK, TOK), columns], dq_out.at[:, out_columns],
+            dq_send_sem.at[h, piece], dq_recv_sem.at[h, group], piece_device(piece),
+        )
+
+    def dq_local(h, piece):
+        columns = pl.ds(pl.multiple_of(h * HEAD, HEAD), HEAD)
+        out_columns = pl.ds(pl.multiple_of(group * QCOLS + h * HEAD, HEAD), HEAD)
+        return pltpu.make_async_copy(
+            dq_send.at[pl.ds(piece * TOK, TOK), columns], dq_out.at[:, out_columns], dq_recv_sem.at[h, group]
+        )
+
+    def finish_head(h):
+        columns = pl.ds(pl.multiple_of(h * HEAD, HEAD), HEAD)
+        dq_send[:, columns] = (dq_t[h].T * REST).astype(BF16)
+        for piece in range(PIECES):
+            pl.when(mine != piece)(lambda: dq_copy(h, piece).start())
+            pl.when(mine == piece)(lambda: dq_local(h, piece).start())
+
+    def far_and_finish(h, carry):
+        pl.when(has_prev2)(lambda: halo(h, far_blocks))
+        finish_head(h)
         return carry
 
-    lax.fori_loop(0, GROUP, own_head, 0)
-
-    def dq_copy(piece):
-        return remote(
-            dq_send.at[pl.ds(piece * TOK, TOK), :], dq_out.at[:, cols(group, QCOLS)],
-            out_send.at[0, piece], out_recv.at[0, group], piece_device(piece),
-        )
-
-    def dq_local(piece):
-        return pltpu.make_async_copy(
-            dq_send.at[pl.ds(piece * TOK, TOK), :], dq_out.at[:, cols(group, QCOLS)], out_recv.at[0, group]
-        )
-
-    def finish_rows(r):
-        rows = pl.ds(r * BLOCK, BLOCK)
-        for h in range(GROUP):
-            dq_send[rows, pl.ds(h * HEAD, HEAD)] = (dq_t[h, :, rows].T * REST).astype(BF16)
-        for piece in (2 * r, 2 * r + 1):
-            pl.when(mine != piece)(lambda: dq_copy(piece).start())
-            pl.when(mine == piece)(lambda: dq_local(piece).start())
+    def early_head(h, carry):
+        wait_head(h)
+        own(h)
+        pl.when(has_prev & (h == 0))(lambda: wait_halo(range(PIECES), 1))
+        pl.when(has_prev)(lambda: halo(h, near_blocks))
+        pl.when(has_prev2 & (h == 1))(lambda: wait_halo(range(Y, PIECES), 2))
+        return lax.fori_loop(h // 2 * 2, h + (h + 1) // 2, far_and_finish, carry)
+
+    lax.fori_loop(0, GROUP - 1, early_head, 0)
 
     def back_copies(j):
         rows = pl.ds(j * BLOCK, BLOCK)
@@ -260,44 +297,35 @@
             for i, (src, dst) in enumerate(((dk_back, dsts[0]), (dv_back, dsts[1])))
         ]
 
-    def halo_block(j):
-        rows = pl.ds(j * BLOCK, BLOCK)
-        far = j * BLOCK < HALF
-        for piece in (2 * j, 2 * j + 1):
-            at = (piece + PIECES) if far else piece - Y
-            at_rows = pl.ds(piece * TOK, TOK)
-            here(k_all.at[at_rows, :], halo_recv.at[0, at]).wait()
-            here(v_all.at[at_rows, :], halo_recv.at[1, at]).wait()
-
-        def head(h, carry):
-            step(j, h, max(0, j - HALO_BLOCKS), min(SPAN_BLOCKS, j + 1))
-            return carry
-
-        lax.fori_loop(0, GROUP, head, 0)
-        dk_back[rows, :] = (dk_acc[rows, :] * REST).astype(BF16)
-        dv_back[rows, :] = (dv_acc[rows, :] * 2.0**SHIFT).astype(BF16)
-        start_all(back_copies(j))
-
-    for j in reversed(range(HALO_BLOCKS)):
-        pl.when(has_prev if j * BLOCK >= HALF else has_prev2)(lambda: halo_block(j))
-        if j < SPAN_BLOCKS:
-            finish_rows(j)
+    def last_halo(blocks):
+        for j in blocks:
+            rows = pl.ds(j * BLOCK, BLOCK)
+            halo(GROUP - 1, (j,))
+            dk_back[rows, :] = (dk_acc[rows, :] * REST).astype(BF16)
+            dv_back[rows, :] = (dv_acc[rows, :] * 2.0**SHIFT).astype(BF16)
+            start_all(back_copies(j))
+
+    wait_head(GROUP - 1)
+    pl.when(has_prev2)(lambda: last_halo(far_blocks))
+    pl.when(has_prev)(lambda: last_halo(near_blocks))
+    own(GROUP - 1)
+    finish_head(GROUP - 1)
 
     def dkv_copies(piece):
         rows = pl.ds(piece * TOK, TOK)
         return [
             remote(
                 src.at[rows, :], dst.at[:, cols(group, HEAD)],
-                out_send.at[i, piece], out_recv.at[i, group], piece_device(piece),
+                dkv_send_sem.at[i, piece], dkv_recv_sem.at[i, group], piece_device(piece),
             )
-            for i, src, dst in ((1, dk_send, dk_out), (2, dv_send, dv_out))
+            for i, src, dst in ((0, dk_send, dk_out), (1, dv_send, dv_out))
         ]
 
     def dkv_local(piece):
         rows = pl.ds(piece * TOK, TOK)
         return [
-            pltpu.make_async_copy(src.at[rows, :], dst.at[:, cols(group, HEAD)], out_recv.at[i, group])
-            for i, src, dst in ((1, dk_send, dk_out), (2, dv_send, dv_out))
+            pltpu.make_async_copy(src.at[rows, :], dst.at[:, cols(group, HEAD)], dkv_recv_sem.at[i, group])
+            for i, src, dst in ((0, dk_send, dk_out), (1, dv_send, dv_out))
         ]
 
     def finish_keys(b):
@@ -326,13 +354,14 @@
             pl.when(mine != piece)(lambda: start_all(dkv_copies(piece)))
             pl.when(mine == piece)(lambda: start_all(dkv_local(piece)))
 
-    for b in (1, 0, 3, 2):
+    for b in reversed(range(SPAN_BLOCKS)):
         finish_keys(b)
 
     for g in range(PIECES):
-        here(dq_out.at[:, pl.ds(g * QCOLS, QCOLS)], out_recv.at[0, g]).wait()
-        here(dk_out.at[:, pl.ds(g * HEAD, HEAD)], out_recv.at[1, g]).wait()
-        here(dv_out.at[:, pl.ds(g * HEAD, HEAD)], out_recv.at[2, g]).wait()
+        for h in range(GROUP):
+            here(dq_out.at[:, pl.ds(g * QCOLS + h * HEAD, HEAD)], dq_recv_sem.at[h, g]).wait()
+        here(dk_out.at[:, pl.ds(g * HEAD, HEAD)], dkv_recv_sem.at[0, g]).wait()
+        here(dv_out.at[:, pl.ds(g * HEAD, HEAD)], dkv_recv_sem.at[1, g]).wait()
     for copy in sends:
         copy.wait_send()
 
@@ -344,14 +373,13 @@
         pl.when(has_next)(lambda: wait_sends(halo_copies(1, piece)))
         if piece >= Y:
             pl.when(has_next2)(lambda: wait_sends(halo_copies(2, piece)))
-        pl.when(mine != piece)(lambda: wait_sends([dq_copy(piece)] + dkv_copies(piece)))
+        pl.when(mine != piece)(lambda: wait_sends([dq_copy(h, piece) for h in range(GROUP)] + dkv_copies(piece)))
     for j in range(HALO_BLOCKS):
         pl.when(has_prev if j * BLOCK >= HALF else has_prev2)(lambda: wait_sends(back_copies(j)))
 
 
 def shards(n_span, query, key, value, out, output_gradient, log_sum_exp, segment_ids):
-    any_space = pl.BlockSpec(memory_space=pl.ANY)
-    vmem = pl.BlockSpec(memory_space=pltpu.VMEM)
+    hbm = pl.BlockSpec(memory_space=pltpu.HBM)
     dma = pltpu.SemaphoreType.DMA
     shape = jax.ShapeDtypeStruct
     window = HALO + SPAN
@@ -362,13 +390,15 @@
             shape(key.shape, BF16),
             shape(value.shape, BF16),
         ],
-        in_specs=[any_space] * 5 + [vmem] * 2,
-        out_specs=[any_space] * 3,
+        in_specs=[hbm] * 7,
+        out_specs=[hbm] * 3,
         scratch_shapes=[
             pltpu.VMEM((TOK, PIECES * HEAD), BF16),
             pltpu.VMEM((TOK, PIECES * HEAD), BF16),
             pltpu.VMEM((TOK, PIECES * QCOLS), BF16),
             pltpu.VMEM((TOK, PIECES * QCOLS), BF16),
+            pltpu.VMEM((PIECES * GROUP, TOK), F32),
+            pltpu.VMEM((segment_ids.shape[0] // TOK, TOK), jnp.int32),
             pltpu.VMEM((PIECES, 2 * GROUP, TOK), F32),
             pltpu.VMEM((window, HEAD), BF16),
             pltpu.VMEM((window, HEAD), BF16),
@@ -389,7 +419,7 @@
             pltpu.VMEM((SPAN, HEAD), BF16),
             pltpu.VMEM((HALF, HEAD), BF16),
             pltpu.VMEM((HALF, HEAD), BF16),
-            dma((4,)),
+            dma((6,)),
             dma((2, PIECES)),
             dma((2, PIECES)),
             dma((PIECES,)),
@@ -400,14 +430,16 @@
             dma((2, PIECES + Y)),
             dma((2, HALO_BLOCKS)),
             dma((2, HALO_BLOCKS)),
-            dma((3, PIECES)),
-            dma((3, PIECES)),
+            dma((GROUP, PIECES)),
+            dma((GROUP, PIECES)),
+            dma((2, PIECES)),
+            dma((2, PIECES)),
         ],
         name="attention_backward",
         compiler_params=pltpu.CompilerParams(
-            collective_id=0, has_side_effects=True, vmem_limit_bytes=48 * 2**20
+            collective_id=0, has_side_effects=True, vmem_limit_bytes=67_043_328
         ),
-    )(query, key, value, out, output_gradient, log_sum_exp, segment_ids.reshape(-1, TOK))
+    )(query, key, value, out, output_gradient, log_sum_exp.T, segment_ids.reshape(-1, TOK))
 
 
 def solution(mesh):

time: 84.1 us -> 75.8 us (0.901)
  the two profiles are of different devices: /device:TPU:103 before, /device:TPU:102 now
where the time goes in v1:
time: 75.8 us; the launch traced here: 75.7 us
  Pallas kernels  70.9 us (94%)
  local copies, waits for them, and re-layouts  4.08 us (5%)
    pallas_call x1, Pallas kernels, shards(): pl.pallas_call(functools.partial(kernel, n_span), out_shape=[shape(query....  70.9 us
    unnamed x7, local copies, waits for them, and re-layouts  4.08 us

profile of v1, /device:TPU:102, one launch (start us, length us, event | category | flops | bytes accessed | tf_op | source)
XLA Modules:
  0.0 75.7 jit_solution(994153672963997243)
XLA Ops:
  0.6 70.9 %attention_backward.1 = (bf16[128,4096]{1,0:T(8,128)(2,1)}, bf16[128,1024]{1,0:T(8,128)(2,1)}, bf16[128,1024]{1,0:T(8,128)(2,1)}) custom-call(bf16[128,4096]{1,0:T(8,128)(2,1)} %q_hbm.1, bf16[128,1024]{1,0:T(8,128)(2,1)} %k_hbm.1, bf16[128,1024]{1,0:T(8,128)(2,1)} %v_hbm.1, bf16[128,4096]{1,0:T(8,128)(2,1)} %o_hbm.1, bf16[128,4096]{1,0:T(8,128)(2,1)} %e_hbm.1, ...), custom_call_target="tpu_custom_call" | custom-call | tf_op jit(solution)/shard_map/attention_backward/pallas_call | solution.py:386
  71.6 0.0 copy-start.1
  71.6 2.3 %copy.13 = bf16[128,4096]{1,0:T(8,128)(2,1)} copy(bf16[128,4096]{1,0:T(8,128)(2,1)} %get-tuple-element.6) | data formatting | bytes 2097152
  73.9 0.0 copy-done.1
  73.9 0.0 copy-start
  73.9 0.7 copy.14
  74.6 0.3 copy-done
  75.0 0.7 copy.15
Async XLA Ops:
  71.6 2.3 %copy-start.1 = (bf16[128,1024]{1,0:T(8,128)(2,1)S(1)}, bf16[128,1024]{1,0:T(8,128)(2,1)}, u32[]{:S(2)}) copy-start(bf16[128,1024]{1,0:T(8,128)(2,1)} %get-tuple-element.7) | copy-start | bytes 786436
  73.9 1.0 %copy-start = (bf16[128,1024]{1,0:T(8,128)(2,1)S(1)}, bf16[128,1024]{1,0:T(8,128)(2,1)}, u32[]{:S(2)}) copy-start(bf16[128,1024]{1,0:T(8,128)(2,1)} %get-tuple-element.8) | copy-start | bytes 786436

commit v2 on v1

--- a/solution.py
+++ b/solution.py
@@ -127,36 +127,45 @@
             )
             sends[-1].start()
 
-    loads[2].wait()
-    for h in range(GROUP):
+    def qe_copies(h):
+        copies = []
         for n, device, g in peers:
             columns = pl.ds(pl.multiple_of(g * QCOLS + h * HEAD, HEAD), HEAD)
+            at_columns = pl.ds(pl.multiple_of(h * HEAD, HEAD), HEAD)
             for i, (src, dst) in enumerate(((q_hbm, q_all), (e_src, e_all))):
-                sends.append(
+                copies.append(
                     remote(
-                        src.at[:, columns], dst.at[my_rows, pl.ds(h * HEAD, HEAD)],
+                        src.at[:, columns], dst.at[my_rows, at_columns],
                         qe_send.at[i, h, n], qe_recv.at[i, h, mine], device,
                     )
                 )
-                sends[-1].start()
-        if h == 0:
-            loads[3].wait()
-            loads[4].wait()
-            lane = lax.broadcasted_iota(jnp.int32, (TOK, HEAD), 1)
-            delta = jnp.zeros((TOK, HEAD), F32)
-            for head in range(PIECES * GROUP):
-                part = pl.ds(head * HEAD, HEAD)
-                product = e_src[:, part].astype(F32) * o_src[:, part].astype(F32)
-                delta = jnp.where(lane == head, jnp.sum(product, axis=1, keepdims=True), delta)
-            delta = delta.T
-            lse = lse_ref[...] * LOG2E + SHIFT
-            for g in range(PIECES):
-                aux_src[g, 0:GROUP, :] = lse[g * GROUP : (g + 1) * GROUP, :]
-                aux_src[g, GROUP : 2 * GROUP, :] = delta[g * GROUP : (g + 1) * GROUP, :]
-            for n, device, g in peers:
-                sends.append(remote(aux_src.at[g], aux.at[mine], aux_send.at[n], aux_recv.at[mine], device))
-                sends[-1].start()
-            aux[mine] = aux_src[group]
+        return copies
+
+    def start_all(copies):
+        for copy in copies:
+            copy.start()
+
+    loads[2].wait()
+    pl.when(core == 0)(lambda: start_all(qe_copies(0)))
+
+    loads[3].wait()
+    loads[4].wait()
+    lane = lax.broadcasted_iota(jnp.int32, (TOK, HEAD), 1)
+    delta = jnp.zeros((TOK, HEAD), F32)
+    for head in range(PIECES * GROUP):
+        part = pl.ds(head * HEAD, HEAD)
+        product = e_src[:, part].astype(F32) * o_src[:, part].astype(F32)
+        delta = jnp.where(lane == head, jnp.sum(product, axis=1, keepdims=True), delta)
+    delta = delta.T
+    lse = lse_ref[...] * LOG2E + SHIFT
+    for g in range(PIECES):
+        aux_src[g, 0:GROUP, :] = lse[g * GROUP : (g + 1) * GROUP, :]
+        aux_src[g, GROUP : 2 * GROUP, :] = delta[g * GROUP : (g + 1) * GROUP, :]
+    for n, device, g in peers:
+        sends.append(remote(aux_src.at[g], aux.at[mine], aux_send.at[n], aux_recv.at[mine], device))
+        sends[-1].start()
+    aux[mine] = aux_src[group]
+    pl.when(core == 0)(lambda: [start_all(qe_copies(h)) for h in range(1, GROUP)] and None)
 
     def halo_copies(by, piece):
         rows = pl.ds(pl.multiple_of(HALO + piece * TOK, TOK), TOK)
@@ -167,10 +176,6 @@
             for i, ref in enumerate((k_all, v_all))
         ]
 
-    def start_all(copies):
-        for copy in copies:
-            copy.start()
-
     def here(ref, sem):
         return pltpu.make_async_copy(ref, ref, sem)
 
@@ -196,12 +201,12 @@
     dv_acc[...] = jnp.zeros_like(dv_acc)
     dq_t[...] = jnp.zeros_like(dq_t)
 
-    for piece in range(PIECES):
+    for piece in range(Y):
         pl.when(mine != piece)(lambda: here(aux.at[piece], aux_recv.at[piece]).wait())
 
-    def step(j, h, r0, r1):
-        keys = pl.ds(j * BLOCK, BLOCK)
-        width = (r1 - r0) * BLOCK
+    def step(j, blocks, h, r0, r1):
+        keys = pl.ds(j * BLOCK, blocks * BLOCK)
+        height, width = blocks * BLOCK, (r1 - r0) * BLOCK
         rows = pl.ds(r0 * BLOCK, width)
         columns = pl.ds(pl.multiple_of(h * HEAD, HEAD), HEAD)
         q, e = q_all[rows, columns], e_all[rows, columns]
@@ -213,9 +218,9 @@
         delta = jnp.concatenate([aux[p, pl.ds(h + GROUP, 1), :] for p in pieces], axis=1)
         doc = jnp.concatenate([seg_k[keys, :]] * (width // TOK), axis=1)
         allowed = doc == seg_q[:, rows]
-        if j >= HALO_BLOCKS:
-            key_at = lax.broadcasted_iota(jnp.int32, (BLOCK, width), 0) + (j - HALO_BLOCKS) * BLOCK
-            query_at = lax.broadcasted_iota(jnp.int32, (BLOCK, width), 1) + r0 * BLOCK
+        if j + blocks - 1 - HALO_BLOCKS >= r0:
+            key_at = lax.broadcasted_iota(jnp.int32, (height, width), 0) + (j - HALO_BLOCKS) * BLOCK
+            query_at = lax.broadcasted_iota(jnp.int32, (height, width), 1) + r0 * BLOCK
             allowed = allowed & (key_at <= query_at)
         probs = jnp.exp2(jnp.where(allowed, scores * (SCALE * LOG2E) - lse, -jnp.inf))
         dscores = (probs * (dprobs - delta)).astype(BF16)
@@ -224,9 +229,9 @@
         dk_acc[keys, :] += jnp.dot(dscores, q, preferred_element_type=F32)
         dq_t[h, :, rows] += lax.dot_general(k, dscores, TN, preferred_element_type=F32)
 
-    def wait_head(h):
+    def wait_head(h, pieces):
         columns = pl.ds(pl.multiple_of(h * HEAD, HEAD), HEAD)
-        for piece in range(PIECES):
+        for piece in pieces:
             rows = pl.ds(piece * TOK, TOK)
             here(q_all.at[rows, columns], qe_recv.at[0, h, piece]).wait()
             here(e_all.at[rows, columns], qe_recv.at[1, h, piece]).wait()
@@ -238,16 +243,17 @@
             here(k_all.at[rows, :], halo_recv.at[0, at]).wait()
             here(v_all.at[rows, :], halo_recv.at[1, at]).wait()
 
-    def own(h):
-        for b in range(SPAN_BLOCKS):
-            step(HALO_BLOCKS + b, h, b, SPAN_BLOCKS)
-
-    def halo(h, blocks):
-        for j in blocks:
-            step(j, h, 0, min(SPAN_BLOCKS, j + 1))
-
-    near_blocks = tuple(reversed(range(HALF // BLOCK, HALO_BLOCKS)))
-    far_blocks = tuple(reversed(range(HALF // BLOCK)))
+    low, high = range(Y), range(Y, PIECES)
+
+    def run(h, steps):
+        for j, blocks, r0, r1 in steps:
+            step(j, blocks, h, r0, r1)
+
+    own_low = ((6, 1, 0, 2), (7, 1, 1, 2))
+    near_low = ((4, 2, 0, 2), (2, 2, 0, 2))
+    far_low = ((1, 1, 0, 2), (0, 1, 0, 1))
+    near_high = ((2, 1, 2, 3), (3, 1, 2, 4), (4, 2, 2, 4))
+    own_high = ((6, 2, 2, 4), (8, 1, 2, 4), (9, 1, 3, 4))
 
     def dq_copy(h, piece):
         columns = pl.ds(pl.multiple_of(h * HEAD, HEAD), HEAD)
@@ -264,27 +270,13 @@
             dq_send.at[pl.ds(piece * TOK, TOK), columns], dq_out.at[:, out_columns], dq_recv_sem.at[h, group]
         )
 
-    def finish_head(h):
+    def finish_head(h, pieces):
         columns = pl.ds(pl.multiple_of(h * HEAD, HEAD), HEAD)
-        dq_send[:, columns] = (dq_t[h].T * REST).astype(BF16)
-        for piece in range(PIECES):
+        rows = pl.ds(pieces[0] * TOK, HALF)
+        dq_send[rows, columns] = (dq_t[h, :, rows].T * REST).astype(BF16)
+        for piece in pieces:
             pl.when(mine != piece)(lambda: dq_copy(h, piece).start())
             pl.when(mine == piece)(lambda: dq_local(h, piece).start())
-
-    def far_and_finish(h, carry):
-        pl.when(has_prev2)(lambda: halo(h, far_blocks))
-        finish_head(h)
-        return carry
-
-    def early_head(h, carry):
-        wait_head(h)
-        own(h)
-        pl.when(has_prev & (h == 0))(lambda: wait_halo(range(PIECES), 1))
-        pl.when(has_prev)(lambda: halo(h, near_blocks))
-        pl.when(has_prev2 & (h == 1))(lambda: wait_halo(range(Y, PIECES), 2))
-        return lax.fori_loop(h // 2 * 2, h + (h + 1) // 2, far_and_finish, carry)
-
-    lax.fori_loop(0, GROUP - 1, early_head, 0)
 
     def back_copies(j):
         rows = pl.ds(j * BLOCK, BLOCK)
@@ -297,19 +289,58 @@
             for i, (src, dst) in enumerate(((dk_back, dsts[0]), (dv_back, dsts[1])))
         ]
 
-    def last_halo(blocks):
-        for j in blocks:
-            rows = pl.ds(j * BLOCK, BLOCK)
-            halo(GROUP - 1, (j,))
-            dk_back[rows, :] = (dk_acc[rows, :] * REST).astype(BF16)
-            dv_back[rows, :] = (dv_acc[rows, :] * 2.0**SHIFT).astype(BF16)
-            start_all(back_copies(j))
-
-    wait_head(GROUP - 1)
-    pl.when(has_prev2)(lambda: last_halo(far_blocks))
-    pl.when(has_prev)(lambda: last_halo(near_blocks))
-    own(GROUP - 1)
-    finish_head(GROUP - 1)
+    def send_back(j, blocks):
+        rows = pl.ds(j * BLOCK, blocks * BLOCK)
+        dk_back[rows, :] = (dk_acc[rows, :] * REST).astype(BF16)
+        dv_back[rows, :] = (dv_acc[rows, :] * 2.0**SHIFT).astype(BF16)
+        for at in range(j, j + blocks):
+            start_all(back_copies(at))
+
+    def low_head(h, carry):
+        wait_head(h, low)
+        pl.when((core == 1) & (h >= 1))(lambda: start_all(qe_copies(h - 1)))
+        run(h, own_low)
+        pl.when(has_prev & (h == 1))(lambda: wait_halo(range(PIECES), 1))
+        pl.when(has_prev & (h >= 1))(lambda: run(h - 1, near_low))
+        return carry
+
+    lax.fori_loop(0, GROUP, low_head, 0)
+    pl.when(core == 1)(lambda: start_all(qe_copies(GROUP - 1)))
+    pl.when(has_prev)(lambda: run(GROUP - 1, near_low))
+    pl.when(has_prev2)(lambda: wait_halo(high, 2))
+
+    def far_head(h, carry):
+        pl.when(has_prev2)(lambda: run(h, far_low))
+        finish_head(h, low)
+        return carry
+
+    lax.fori_loop(0, GROUP, far_head, 0)
+    pl.when(has_prev2)(lambda: send_back(0, 2))
+
+    for piece in high:
+        pl.when(mine != piece)(lambda: here(aux.at[piece], aux_recv.at[piece]).wait())
+
+    def near_head(h, carry):
+        wait_head(h, high)
+        pl.when(has_prev)(lambda: run(h, near_high))
+        return carry
+
+    lax.fori_loop(0, GROUP - 1, near_head, 0)
+    wait_head(GROUP - 1, high)
+
+    def last_near():
+        for j, blocks, r0, r1 in near_high:
+            step(j, blocks, GROUP - 1, r0, r1)
+            send_back(j, blocks)
+
+    pl.when(has_prev)(last_near)
+
+    def high_head(h, carry):
+        run(h, own_high)
+        finish_head(h, high)
+        return carry
+
+    lax.fori_loop(0, GROUP, high_head, 0)
 
     def dkv_copies(piece):
         rows = pl.ds(piece * TOK, TOK)
@@ -354,7 +385,7 @@
             pl.when(mine != piece)(lambda: start_all(dkv_copies(piece)))
             pl.when(mine == piece)(lambda: start_all(dkv_local(piece)))
 
-    for b in reversed(range(SPAN_BLOCKS)):
+    for b in range(SPAN_BLOCKS):
         finish_keys(b)
 
     for g in range(PIECES):
@@ -362,12 +393,13 @@
             here(dq_out.at[:, pl.ds(g * QCOLS + h * HEAD, HEAD)], dq_recv_sem.at[h, g]).wait()
         here(dk_out.at[:, pl.ds(g * HEAD, HEAD)], dkv_recv_sem.at[0, g]).wait()
         here(dv_out.at[:, pl.ds(g * HEAD, HEAD)], dkv_recv_sem.at[1, g]).wait()
-    for copy in sends:
-        copy.wait_send()
-
     def wait_sends(copies):
         for copy in copies:
             copy.wait_send()
+
+    wait_sends(sends)
+    for h in range(GROUP):
+        wait_sends(qe_copies(h))
 
     for piece in range(PIECES):
         pl.when(has_next)(lambda: wait_sends(halo_copies(1, piece)))

time: 75.8 us -> 69.1 us (0.912)
  the two profiles are of different devices: /device:TPU:102 before, /device:TPU:103 now
where the time goes in v2:
time: 69.1 us; the launch traced here: 68.9 us
  Pallas kernels  64.2 us (93%)
  local copies, waits for them, and re-layouts  4.08 us (6%)
    pallas_call x1, Pallas kernels, shards(): pl.pallas_call(functools.partial(kernel, n_span), out_shape=[shape(query....  64.2 us
    unnamed x7, local copies, waits for them, and re-layouts  4.08 us

profile of v2, /device:TPU:103, one launch (start us, length us, event | category | flops | bytes accessed | tf_op | source)
XLA Modules:
  0.0 68.9 jit_solution(11047415372095545679)
XLA Ops:
  0.6 64.2 %attention_backward.1 = (bf16[128,4096]{1,0:T(8,128)(2,1)}, bf16[128,1024]{1,0:T(8,128)(2,1)}, bf16[128,1024]{1,0:T(8,128)(2,1)}) custom-call(bf16[128,4096]{1,0:T(8,128)(2,1)} %q_hbm.1, bf16[128,1024]{1,0:T(8,128)(2,1)} %k_hbm.1, bf16[128,1024]{1,0:T(8,128)(2,1)} %v_hbm.1, bf16[128,4096]{1,0:T(8,128)(2,1)} %o_hbm.1, bf16[128,4096]{1,0:T(8,128)(2,1)} %e_hbm.1, ...), custom_call_target="tpu_custom_call" | custom-call | tf_op jit(solution)/shard_map/attention_backward/pallas_call | solution.py:418
  64.8 0.0 copy-start.1
  64.8 2.3 %copy.13 = bf16[128,4096]{1,0:T(8,128)(2,1)} copy(bf16[128,4096]{1,0:T(8,128)(2,1)} %get-tuple-element.6) | data formatting | bytes 2097152
  67.1 0.0 copy-done.1
  67.1 0.0 copy-start
  67.1 0.7 %copy.14 = bf16[128,1024]{1,0:T(8,128)(2,1)} copy(bf16[128,1024]{1,0:T(8,128)(2,1)S(1)} %copy-done.1) | data formatting | bytes 524288
  67.8 0.3 copy-done
  68.2 0.7 %copy.15 = bf16[128,1024]{1,0:T(8,128)(2,1)} copy(bf16[128,1024]{1,0:T(8,128)(2,1)S(1)} %copy-done) | data formatting | bytes 524288
Async XLA Ops:
  64.8 2.3 %copy-start.1 = (bf16[128,1024]{1,0:T(8,128)(2,1)S(1)}, bf16[128,1024]{1,0:T(8,128)(2,1)}, u32[]{:S(2)}) copy-start(bf16[128,1024]{1,0:T(8,128)(2,1)} %get-tuple-element.7) | copy-start | bytes 786436
  67.1 1.0 %copy-start = (bf16[128,1024]{1,0:T(8,128)(2,1)S(1)}, bf16[128,1024]{1,0:T(8,128)(2,1)}, u32[]{:S(2)}) copy-start(bf16[128,1024]{1,0:T(8,128)(2,1)} %get-tuple-element.8) | copy-start | bytes 786436

commit v3 on v2

--- a/solution.py
+++ b/solution.py
@@ -204,15 +204,20 @@
     for piece in range(Y):
         pl.when(mine != piece)(lambda: here(aux.at[piece], aux_recv.at[piece]).wait())
 
-    def step(j, blocks, h, r0, r1):
+    def where(j, blocks, h, r0, r1):
         keys = pl.ds(j * BLOCK, blocks * BLOCK)
+        rows = pl.ds(r0 * BLOCK, (r1 - r0) * BLOCK)
+        return keys, rows, pl.ds(pl.multiple_of(h * HEAD, HEAD), HEAD)
+
+    def products(j, blocks, h, r0, r1):
+        keys, rows, columns = where(j, blocks, h, r0, r1)
+        scores = lax.dot_general(k_all[keys, :], q_all[rows, columns], NT, preferred_element_type=F32)
+        dprobs = lax.dot_general(v_all[keys, :], e_all[rows, columns], NT, preferred_element_type=F32)
+        return scores, dprobs
+
+    def softmax_grad(j, blocks, h, r0, r1, scores, dprobs):
+        keys, rows, _ = where(j, blocks, h, r0, r1)
         height, width = blocks * BLOCK, (r1 - r0) * BLOCK
-        rows = pl.ds(r0 * BLOCK, width)
-        columns = pl.ds(pl.multiple_of(h * HEAD, HEAD), HEAD)
-        q, e = q_all[rows, columns], e_all[rows, columns]
-        k, v = k_all[keys, :], v_all[keys, :]
-        scores = lax.dot_general(k, q, NT, preferred_element_type=F32)
-        dprobs = lax.dot_general(v, e, NT, preferred_element_type=F32)
         pieces = range(r0 * BLOCK // TOK, r1 * BLOCK // TOK)
         lse = jnp.concatenate([aux[p, pl.ds(h, 1), :] for p in pieces], axis=1)
         delta = jnp.concatenate([aux[p, pl.ds(h + GROUP, 1), :] for p in pieces], axis=1)
@@ -223,11 +228,13 @@
             query_at = lax.broadcasted_iota(jnp.int32, (height, width), 1) + r0 * BLOCK
             allowed = allowed & (key_at <= query_at)
         probs = jnp.exp2(jnp.where(allowed, scores * (SCALE * LOG2E) - lse, -jnp.inf))
-        dscores = (probs * (dprobs - delta)).astype(BF16)
-        probs = probs.astype(BF16)
-        dv_acc[keys, :] += jnp.dot(probs, e, preferred_element_type=F32)
-        dk_acc[keys, :] += jnp.dot(dscores, q, preferred_element_type=F32)
-        dq_t[h, :, rows] += lax.dot_general(k, dscores, TN, preferred_element_type=F32)
+        return probs.astype(BF16), (probs * (dprobs - delta)).astype(BF16)
+
+    def gradients(j, blocks, h, r0, r1, probs, dscores):
+        keys, rows, columns = where(j, blocks, h, r0, r1)
+        dv_acc[keys, :] += jnp.dot(probs, e_all[rows, columns], preferred_element_type=F32)
+        dk_acc[keys, :] += jnp.dot(dscores, q_all[rows, columns], preferred_element_type=F32)
+        dq_t[h, :, rows] += lax.dot_general(k_all[keys, :], dscores, TN, preferred_element_type=F32)
 
     def wait_head(h, pieces):
         columns = pl.ds(pl.multiple_of(h * HEAD, HEAD), HEAD)
@@ -245,15 +252,23 @@
 
     low, high = range(Y), range(Y, PIECES)
 
-    def run(h, steps):
-        for j, blocks, r0, r1 in steps:
-            step(j, blocks, h, r0, r1)
-
-    own_low = ((6, 1, 0, 2), (7, 1, 1, 2))
-    near_low = ((4, 2, 0, 2), (2, 2, 0, 2))
-    far_low = ((1, 1, 0, 2), (0, 1, 0, 1))
-    near_high = ((2, 1, 2, 3), (3, 1, 2, 4), (4, 2, 2, 4))
-    own_high = ((6, 2, 2, 4), (8, 1, 2, 4), (9, 1, 3, 4))
+    def run(h, steps, after=None):
+        steps = [(j, blocks, h, r0, r1) for j, blocks, r0, r1 in steps]
+        ready = products(*steps[0])
+        for i, at in enumerate(steps):
+            low_types = softmax_grad(*at, *ready)
+            if i + 1 < len(steps):
+                ready = products(*steps[i + 1])
+            gradients(*at, *low_types)
+            if after:
+                after(at[0], at[1])
+
+    own_low = ((6, 1, 0, 1), (6, 2, 1, 2))
+    near_low = ((2, 4, 0, 1), (2, 4, 1, 2))
+    far_low = ((0, 2, 0, 1), (1, 1, 1, 2))
+    near_high = ((2, 4, 2, 3), (3, 3, 3, 4))
+    own_high = ((6, 3, 2, 3), (6, 4, 3, 4))
+    last_near = ((2, 1, 2, 3), (3, 1, 2, 4), (4, 2, 2, 4))
 
     def dq_copy(h, piece):
         columns = pl.ds(pl.multiple_of(h * HEAD, HEAD), HEAD)
@@ -328,12 +343,7 @@
     lax.fori_loop(0, GROUP - 1, near_head, 0)
     wait_head(GROUP - 1, high)
 
-    def last_near():
-        for j, blocks, r0, r1 in near_high:
-            step(j, blocks, GROUP - 1, r0, r1)
-            send_back(j, blocks)
-
-    pl.when(has_prev)(last_near)
+    pl.when(has_prev)(lambda: run(GROUP - 1, last_near, send_back))
 
     def high_head(h, carry):
         run(h, own_high)
@@ -410,12 +420,23 @@
         pl.when(has_prev if j * BLOCK >= HALF else has_prev2)(lambda: wait_sends(back_copies(j)))
 
 
+def store(*refs):
+    sems = refs[-1]
+    copies = [pltpu.make_async_copy(refs[i], refs[i + 3], sems.at[i]) for i in range(3)]
+    for copy in copies:
+        copy.start()
+    for copy in copies:
+        copy.wait()
+
+
 def shards(n_span, query, key, value, out, output_gradient, log_sum_exp, segment_ids):
     hbm = pl.BlockSpec(memory_space=pltpu.HBM)
     dma = pltpu.SemaphoreType.DMA
     shape = jax.ShapeDtypeStruct
     window = HALO + SPAN
-    return pl.pallas_call(
+    args = (query, key, value, out, output_gradient, log_sum_exp.T, segment_ids.reshape(-1, TOK))
+    args = [pltpu.with_memory_space_constraint(a, pltpu.HBM) for a in args]
+    grads = pl.pallas_call(
         functools.partial(kernel, n_span),
         out_shape=[
             shape(query.shape, BF16),
@@ -469,9 +490,17 @@
         ],
         name="attention_backward",
         compiler_params=pltpu.CompilerParams(
-            collective_id=0, has_side_effects=True, vmem_limit_bytes=67_043_328
+            collective_id=0, has_side_effects=True, vmem_limit_bytes=40 * 2**20
         ),
-    )(query, key, value, out, output_gradient, log_sum_exp.T, segment_ids.reshape(-1, TOK))
+    )(*args)
+    return pl.pallas_call(
+        store,
+        out_shape=[shape(g.shape, BF16) for g in grads],
+        in_specs=[pl.BlockSpec(memory_space=pltpu.VMEM)] * 3,
+        out_specs=[hbm] * 3,
+        scratch_shapes=[dma((3,))],
+        name="store_gradients",
+    )(*[pltpu.with_memory_space_constraint(g, pltpu.VMEM) for g in grads])
 
 
 def solution(mesh):

time: 69.1 us -> 64.4 us (0.932)
  local copies, waits for them, and re-layouts: 4.08 us -> 0 us
    unnamed x7 -> x0, local copies, waits for them, and re-layouts: 4.08 us -> none
    pallas_call x1, Pallas kernels: 64.2 us -> 62.5 us  [shards(): pl.pallas_call(functools.partial(kernel, n_span), out_shape=[shape(query....]
    pallas_call x0 -> x1, Pallas kernels: none -> 1.16 us  [shards(): pl.pallas_call(store, out_shape=[shape(g.shape, BF16) for g in grads], in...]
where the time goes in v3:
time: 64.4 us; the launch traced here: 64.3 us
  Pallas kernels  63.6 us (99%)
    pallas_call x1, Pallas kernels, shards(): pl.pallas_call(functools.partial(kernel, n_span), out_shape=[shape(query....  62.5 us

profile of v3, /device:TPU:103, one launch (start us, length us, event | category | flops | bytes accessed | tf_op | source)
XLA Modules:
  0.0 64.3 jit_solution(8257793218320508671)
XLA Ops:
  0.6 62.5 %attention_backward.1 = (bf16[128,4096]{1,0:T(8,128)(2,1)S(1)}, bf16[128,1024]{1,0:T(8,128)(2,1)S(1)}, bf16[128,1024]{1,0:T(8,128)(2,1)S(1)}) custom-call(bf16[128,4096]{1,0:T(8,128)(2,1)} %q_hbm.1, bf16[128,1024]{1,0:T(8,128)(2,1)} %k_hbm.1, bf16[128,1024]{1,0:T(8,128)(2,1)} %v_hbm.1, bf16[128,4096]{1,0:T(8,128)(2,1)} %o_hbm.1, bf16[128,4096]{1,0:T(8,128)(2,1)} %e_hbm.1, ...), custom_call_target="tpu_custom_call" | custom-call | tf_op jit(solution)/shard_map/attention_backward/pallas_call | solution.py:439
  63.1 1.2 %store_gradients.1 = (bf16[128,4096]{1,0:T(8,128)(2,1)}, bf16[128,1024]{1,0:T(8,128)(2,1)}, bf16[128,1024]{1,0:T(8,128)(2,1)}) custom-call(bf16[128,4096]{1,0:T(8,128)(2,1)S(1)} %get-tuple-element.6.refs_0_, bf16[128,1024]{1,0:T(8,128)(2,1)S(1)} %get-tuple-element.7.refs_1_, bf16[128,1024]{1,0:T(8,128)(2,1)S(1)} %get-tuple-element.8.refs_2_), custom_call_target="tpu_custom_call" | custom-call | tf_op jit(solution)/shard_map/store_gradients/pallas_call | solution.py:496

commit v4 on v3

--- a/solution.py
+++ b/solution.py
@@ -59,8 +59,8 @@
         return (seq + 2 * by, y)
 
     peers = []
-    for dy in (1, 3, 2, 0):
-        for dcore in (0, 1):
+    for dy in (1, 3, 0, 2):
+        for dcore in (1, 0):
             if dy or dcore:
                 py = lax.rem(y + dy, Y)
                 pcore = lax.rem(core + dcore, 2)

time: 64.4 us -> 63.8 us (level)
  Pallas kernels: 63.6 us -> 62.7 us
    pallas_call x1, Pallas kernels: 62.5 us -> 61.6 us  [shards(): pl.pallas_call(functools.partial(kernel, n_span), out_shape=[shape(query....]
where the time goes in v4:
time: 63.8 us; the launch traced here: 63.4 us
  Pallas kernels  62.7 us (98%)
  between operations  0.64 us (1%)
    pallas_call x1, Pallas kernels, shards(): pl.pallas_call(functools.partial(kernel, n_span), out_shape=[shape(query....  61.6 us

profile of v4, /device:TPU:103, one launch (start us, length us, event | category | flops | bytes accessed | tf_op | source)
XLA Modules:
  0.0 63.4 jit_solution(6843193294791368986)
XLA Ops:
  0.6 61.6 %attention_backward.1 = (bf16[128,4096]{1,0:T(8,128)(2,1)S(1)}, bf16[128,1024]{1,0:T(8,128)(2,1)S(1)}, bf16[128,1024]{1,0:T(8,128)(2,1)S(1)}) custom-call(bf16[128,4096]{1,0:T(8,128)(2,1)} %q_hbm.1, bf16[128,1024]{1,0:T(8,128)(2,1)} %k_hbm.1, bf16[128,1024]{1,0:T(8,128)(2,1)} %v_hbm.1, bf16[128,4096]{1,0:T(8,128)(2,1)} %o_hbm.1, bf16[128,4096]{1,0:T(8,128)(2,1)} %e_hbm.1, ...), custom_call_target="tpu_custom_call" | custom-call | tf_op jit(solution)/shard_map/attention_backward/pallas_call | solution.py:439
  62.2 1.2 %store_gradients.1 = (bf16[128,4096]{1,0:T(8,128)(2,1)}, bf16[128,1024]{1,0:T(8,128)(2,1)}, bf16[128,1024]{1,0:T(8,128)(2,1)}) custom-call(bf16[128,4096]{1,0:T(8,128)(2,1)S(1)} %get-tuple-element.6.refs_0_, bf16[128,1024]{1,0:T(8,128)(2,1)S(1)} %get-tuple-element.7.refs_1_, bf16[128,1024]{1,0:T(8,128)(2,1)S(1)} %get-tuple-element.8.refs_2_), custom_call_target="tpu_custom_call" | custom-call | tf_op jit(solution)/shard_map/store_gradients/pallas_call | solution.py:496

commit v5 on v4

--- a/solution.py
+++ b/solution.py
@@ -37,7 +37,7 @@
     n_span,
     q_hbm, k_hbm, v_hbm, o_hbm, e_hbm, lse_hbm, seg_hbm,
     dq_out, dk_out, dv_out,
-    k_src, v_src, o_src, e_src, lse_ref, seg_ref, aux_src,
+    k_src, v_src, o_src, e_src, q_src, lse_ref, seg_ref, aux_src,
     k_all, v_all, q_all, e_all, aux, seg_k, seg_q,
     dq_t, dk_acc, dv_acc,
     dq_send, dk_send, dv_send, dk_back, dv_back, dk_near, dv_near, dk_far, dv_far,
@@ -79,7 +79,7 @@
         for i, (src, dst) in enumerate(
             (
                 (k_hbm, k_src), (v_hbm, v_src), (e_hbm, e_src), (o_hbm, o_src),
-                (lse_hbm, lse_ref), (seg_hbm, seg_ref),
+                (lse_hbm, lse_ref), (seg_hbm, seg_ref), (q_hbm, q_src),
             )
         )
     ]
@@ -132,7 +132,7 @@
         for n, device, g in peers:
             columns = pl.ds(pl.multiple_of(g * QCOLS + h * HEAD, HEAD), HEAD)
             at_columns = pl.ds(pl.multiple_of(h * HEAD, HEAD), HEAD)
-            for i, (src, dst) in enumerate(((q_hbm, q_all), (e_src, e_all))):
+            for i, (src, dst) in enumerate(((q_src, q_all), (e_src, e_all))):
                 copies.append(
                     remote(
                         src.at[:, columns], dst.at[my_rows, at_columns],
@@ -146,6 +146,7 @@
             copy.start()
 
     loads[2].wait()
+    loads[6].wait()
     pl.when(core == 0)(lambda: start_all(qe_copies(0)))
 
     loads[3].wait()
@@ -179,7 +180,7 @@
     def here(ref, sem):
         return pltpu.make_async_copy(ref, ref, sem)
 
-    for dy, dcore in ((0, 0), (0, 1), (1, 0), (3, 0), (1, 1), (3, 1), (2, 0), (2, 1)):
+    for dy, dcore in ((0, 0), (0, 1), (1, 1), (3, 1), (1, 0), (3, 0), (2, 1), (2, 0)):
         piece = lax.rem(core + dcore, 2) * Y + lax.rem(y + dy, Y)
         rows = pl.ds(pl.multiple_of(HALO + piece * TOK, TOK), TOK)
         here(k_all.at[rows, :], kv_recv.at[0, piece]).wait()
@@ -448,6 +449,7 @@
         scratch_shapes=[
             pltpu.VMEM((TOK, PIECES * HEAD), BF16),
             pltpu.VMEM((TOK, PIECES * HEAD), BF16),
+            pltpu.VMEM((TOK, PIECES * QCOLS), BF16),
             pltpu.VMEM((TOK, PIECES * QCOLS), BF16),
             pltpu.VMEM((TOK, PIECES * QCOLS), BF16),
             pltpu.VMEM((PIECES * GROUP, TOK), F32),
@@ -472,7 +474,7 @@
             pltpu.VMEM((SPAN, HEAD), BF16),
             pltpu.VMEM((HALF, HEAD), BF16),
             pltpu.VMEM((HALF, HEAD), BF16),
-            dma((6,)),
+            dma((7,)),
             dma((2, PIECES)),
             dma((2, PIECES)),
             dma((PIECES,)),

time: 63.8 us -> 64.7 us (1.014)
  Pallas kernels: 62.7 us -> 64 us
    pallas_call x1, Pallas kernels: 61.6 us -> 62.8 us  [shards(): pl.pallas_call(functools.partial(kernel, n_span), out_shape=[shape(query....]
where the time goes in v5:
time: 64.7 us
  Pallas kernels  64 us (99%)
    pallas_call x1, Pallas kernels, shards(): pl.pallas_call(functools.partial(kernel, n_span), out_shape=[shape(query....  62.8 us

profile of v5, /device:TPU:103, one launch (start us, length us, event | category | flops | bytes accessed | tf_op | source)
XLA Modules:
  0.0 64.7 jit_solution(9011770884249220228)
XLA Ops:
  0.6 62.8 %attention_backward.1 = (bf16[128,4096]{1,0:T(8,128)(2,1)S(1)}, bf16[128,1024]{1,0:T(8,128)(2,1)S(1)}, bf16[128,1024]{1,0:T(8,128)(2,1)S(1)}) custom-call(bf16[128,4096]{1,0:T(8,128)(2,1)} %q_hbm.1, bf16[128,1024]{1,0:T(8,128)(2,1)} %k_hbm.1, bf16[128,1024]{1,0:T(8,128)(2,1)} %v_hbm.1, bf16[128,4096]{1,0:T(8,128)(2,1)} %o_hbm.1, bf16[128,4096]{1,0:T(8,128)(2,1)} %e_hbm.1, ...), custom_call_target="tpu_custom_call" | custom-call | tf_op jit(solution)/shard_map/attention_backward/pallas_call | solution.py:440
  63.5 1.2 %store_gradients.1 = (bf16[128,4096]{1,0:T(8,128)(2,1)}, bf16[128,1024]{1,0:T(8,128)(2,1)}, bf16[128,1024]{1,0:T(8,128)(2,1)}) custom-call(bf16[128,4096]{1,0:T(8,128)(2,1)S(1)} %get-tuple-element.6.refs_0_, bf16[128,1024]{1,0:T(8,128)(2,1)S(1)} %get-tuple-element.7.refs_1_, bf16[128,1024]{1,0:T(8,128)(2,1)S(1)} %get-tuple-element.8.refs_2_), custom_call_target="tpu_custom_call" | custom-call | tf_op jit(solution)/shard_map/store_gradients/pallas_call | solution.py:498
